TPU v7x, 8 devices: a whole 2x2x1 slice. The times are simulated.
8 devices in a mesh: cp: 8 (over z, y, x, core).
Axes of the slice: x: 2, y: 2, z: 1, core: 2. Of those that a mesh axis runs over, the one named last changes fastest.
Arguments:
- x_in: bfloat16 [8192, 640], P('cp')
- norm_gains: float32 [2, 4, 640], replicated
- qk_gains: float32 [2, 2, 256], replicated
- w_q: bfloat16 [2, 640, 4, 256], replicated
- w_k: bfloat16 [2, 640, 1, 256], replicated
- w_v: bfloat16 [2, 640, 1, 256], replicated
- w_o: bfloat16 [2, 4, 256, 640], replicated
- w_gate: bfloat16 [2, 640, 2048], replicated
- w_up: bfloat16 [2, 640, 2048], replicated
- w_down: bfloat16 [2, 2048, 640], replicated
Outputs:
- output 1: bfloat16 [8192, 640], P('cp')
- output 2: bfloat16 [8192, 1, 256], P('cp')
- output 3: bfloat16 [8192, 1, 256], P('cp')
- output 4: bfloat16 [1024, 1, 256], replicated
- output 5: bfloat16 [1024, 1, 256], replicated
All inputs are finite; a program needn't handle non-finite values.
Results may differ from a plain program's by a relative error of at most 0.016197.
Values are sent between devices in bfloat16 or wider.
A program may use at most 1 GiB of HBM per device.

v0:
```python
import functools

import numpy as np
import jax
import jax.numpy as jnp
from jax import lax
from jax.experimental import pallas as pl
from jax.experimental.pallas import tpu as pltpu
from jax.sharding import PartitionSpec as P

WINDOW = 1024
EPS = 1e-6
BASES = (10000.0, 1000000.0)
SCALES = (1.0, 8.0)
HEAD = 256
TOK = 1024
D = 640
FF = 2048
TILE = 256
LO = 32
LOG2E = 1.4426950408889634
COEF = LOG2E / 16.0
TOP = 36.0
LIMIT = 56.0
NEG = -1e30
F32 = jnp.float32
BF16 = jnp.bfloat16
VLIM = 58 << 20


def rope_const(layer, seq_len):
    base, scale = BASES[layer], SCALES[layer]
    freq = base ** (-np.arange(HEAD // 2, dtype=np.float64) * 2.0 / HEAD)
    hi = (np.arange(seq_len // LO) * LO / scale)[:, None] * freq[None, :]
    lo = (np.arange(LO) / scale)[:, None] * freq[None, :]
    hi_tab = np.concatenate([np.cos(hi), np.sin(hi)], axis=1).astype(np.float32)
    lo_tab = np.concatenate([np.cos(lo), np.sin(lo)], axis=1).astype(np.float32)
    return hi_tab, lo_tab


def rms(x, gain):
    return x * lax.rsqrt(jnp.mean(x * x, axis=-1, keepdims=True) + EPS) * gain


def cos_sin(hi_ref, lo_ref, row0, rows):
    n_hi = rows // LO
    hi = hi_ref[pl.ds(pl.multiple_of(row0 // LO, 8), n_hi), :]
    lo = lo_ref[...]
    ch, sh = hi[:, None, 0:128], hi[:, None, 128:256]
    cl, sl = lo[None, :, 0:128], lo[None, :, 128:256]
    cos = (ch * cl - sh * sl).reshape(rows, 128)
    sin = (sh * cl + ch * sl).reshape(rows, 128)
    return cos, sin


def rotate(x, cos, sin):
    a, b = x[:, 0:128], x[:, 128:256]
    return jnp.concatenate([a * cos - b * sin, b * cos + a * sin], axis=1).astype(BF16)


def head_rope(proj, gain, cos, sin):
    return rotate(rms(proj.astype(BF16).astype(F32), gain), cos, sin)


def dot(a, b):
    return jnp.dot(a, b, preferred_element_type=F32)


def dot_t(a, b):
    return lax.dot_general(a, b, (((1,), (1,)), ((), ())), preferred_element_type=F32)


MESH = pl.DeviceIdType.MESH
N_SLOT = 8
OWN = 7
LENT = 256
N_TILE = TOK // TILE
QROWS = 512
FROWS = 512


def finish_rows(fast, x, attn, ng, wo, wg, wu, wd):
    o = dot(attn, wo[...]).astype(BF16).astype(F32)
    h1 = (x.astype(F32) + rms(o, 1.0 + ng[1:2, :])).astype(BF16)
    b = rms(h1.astype(F32), 1.0 + ng[2:3, :]).astype(BF16)

    def ff(cols):
        m = (jax.nn.gelu(dot(b, wg[:, cols]), approximate=True) * dot(b, wu[:, cols])).astype(BF16)
        return dot(m, wd[cols, :])

    if fast:
        acc = ff(slice(None))
    else:
        acc = lax.fori_loop(0, FF // 256, lambda f, part: part + ff(pl.ds(pl.multiple_of(f * 256, 256), 256)), jnp.zeros(h1.shape, F32))
    o2 = acc.astype(BF16).astype(F32)
    return (h1.astype(F32) + rms(o2, 1.0 + ng[3:4, :])).astype(BF16)


def layers_kernel(fast, ng_ref, qg_ref, hi4_ref, lo4_ref, hi5_ref, lo5_ref, x_hbm, wq_hbm, wk_hbm, wv_hbm, wo_hbm, wg_hbm, wu_hbm, wd_hbm,
                  out_hbm, k_hbm, v_hbm, kl_hbm, vl_hbm, bound_ref,
                  x, mid, win, q, buf, acc, l, m, lent, last, xo, wq, wk, wv, wo, wg, wu, wd,
                  load_sem, out_sem, halo_send, halo_recv, hop_send, hop_recv, pass_send, over_send, wide_recv, last_send, last_recv, lend_sem):
    me = lax.axis_index('cp')
    core = me % 2
    chip = me // 2
    partner = me + 1 - 2 * core
    xnb = me + 2 - 4 * (chip % 2)
    ynb = me + 4 - 8 * (chip // 2)
    top = 7
    is_last = me == top
    kv5 = buf.at[OWN]
    near, helper, far = chip == 0, chip == 1, chip == 3
    borrowed = pl.ds(TOK, LENT)

    def load(src, dst, n):
        return pltpu.make_async_copy(src, dst, load_sem.at[n])

    early = [load(x_hbm, x, 0), load(wk_hbm.at[0], wk.at[0], 1), load(wv_hbm.at[0], wv.at[0], 2), load(wq_hbm.at[0], wq.at[0], 3)]
    ff4 = [load(wo_hbm.at[0], wo, 4), load(wg_hbm.at[0], wg, 5), load(wu_hbm.at[0], wu, 6), load(wd_hbm.at[0], wd, 7)]
    next_qkv = [load(wk_hbm.at[1], wk.at[1], 8), load(wv_hbm.at[1], wv.at[1], 9), load(wq_hbm.at[1], wq.at[1], 10)]
    ff5 = [load(wo_hbm.at[1], wo, 4), load(wg_hbm.at[1], wg, 5), load(wu_hbm.at[1], wu, 6), load(wd_hbm.at[1], wd, 7)]
    for cp in early:
        cp.start()

    if fast:
        barrier = pltpu.get_barrier_semaphore()
        for other in (partner, xnb, ynb, (me + 1) % 8, (me + 7) % 8):
            pl.semaphore_signal(barrier, inc=1, device_id=(other,), device_id_type=MESH)
    for cp in ff4 + next_qkv:
        cp.start()

    @pl.when(me == 0)
    def _():
        win[0:WINDOW, :] = jnp.zeros((WINDOW, 2 * HEAD), BF16)

    if fast:
        pl.semaphore_wait(barrier, 5)

    def send(src, dst, ssem, rsem, dev):
        return pltpu.make_async_remote_copy(src_ref=src, dst_ref=dst, send_sem=ssem, recv_sem=rsem, device_id=(dev,), device_id_type=MESH)

    def heads(one):
        if fast:
            for h in range(4):
                one(h, 0)
        else:
            lax.fori_loop(0, 4, one, 0)

    def on(cond, copy, act):
        @pl.when(cond)
        def _():
            getattr(copy, act)()

    def rows_of(t, n=TILE):
        return pl.ds(pl.multiple_of(t * n, n), n)

    def halo_copy(t):
        return send(win.at[rows_of(t + N_TILE)], win.at[rows_of(t)], halo_send.at[t], halo_recv.at[t], (me + 1) % 8)

    gains = jnp.abs(1.0 + qg_ref[...])
    pair = jnp.maximum(gains[:, :, 0:HEAD // 2], gains[:, :, HEAD // 2:])
    bound = 16.0 * 1.02 * jnp.max(pair[:, 0:1] * pair[:, 1:2])
    bound_ref[0] = bound
    sigma = jnp.maximum(bound - TOP, 0.0) * LOG2E
    g4q, g4k = 1.0 + qg_ref[0, 0:1, :], 1.0 + qg_ref[0, 1:2, :]
    g5q, g5k = 1.0 + qg_ref[1, 0:1, :], 1.0 + qg_ref[1, 1:2, :]
    for cp in early[:3]:
        cp.wait()

    def kv_tile(it, carry):
        t = N_TILE - 1 - it
        cos, sin = cos_sin(hi4_ref, lo4_ref, me * TOK + t * TILE, TILE)
        a = rms(x[rows_of(t), :].astype(F32), 1.0 + ng_ref[0, 0:1, :]).astype(BF16)
        win[rows_of(t + N_TILE), 0:HEAD] = head_rope(dot(a, wk[0]), g4k, cos, sin)
        win[rows_of(t + N_TILE), HEAD:2 * HEAD] = dot(a, wv[0]).astype(BF16)
        on(me < top, halo_copy(t), 'start')
        return carry

    lax.fori_loop(0, N_TILE, kv_tile, 0)
    own4 = win.at[pl.ds(WINDOW, TOK)]
    last_cps = [send(own4, last, last_send.at[n], last_recv, dev) for n, dev in enumerate((partner, xnb, ynb))]
    for cp in last_cps:
        on(is_last, cp, 'start')
    early[3].wait()
    for cp in ff4 + next_qkv:
        cp.wait()

    def hops(t):
        def hop(k, slot, rk, dev):
            return send(kv5.at[rows_of(t)], buf.at[slot, rows_of(t)], hop_send.at[k, t], hop_recv.at[rk, t], dev)
        return [(jnp.logical_or(core == 0, helper), hop(0, 0, 0, partner)),
                (chip == 0, hop(1, 1, 1, xnb)),
                (chip == 0, hop(2, 1, 1, ynb)),
                (chip == 1, hop(2, 1, 1, ynb)),
                (chip == 2, hop(1, 3, 2, xnb)),
                (me == 5, hop(2, 3, 2, ynb)),
                (me == 6, hop(2, 5, 3, ynb)),
                (jnp.logical_and(me == 7, t == 0), hop(2, 6, 3, ynb))]

    def early_pass(t):
        return send(buf.at[1, rows_of(t)], buf.at[3, rows_of(t)], hop_send.at[3, t], hop_recv.at[2, t], xnb)

    def first_in(t):
        send(kv5.at[rows_of(t)], buf.at[1, rows_of(t)], hop_send.at[0, t], hop_recv.at[1, t], partner).wait_recv()

    def third_in(t):
        send(kv5.at[rows_of(t)], buf.at[3, rows_of(t)], hop_send.at[0, t], hop_recv.at[2, t], partner).wait_recv()

    def over_pass(k, t, dev):
        return send(buf.at[3, rows_of(t)], buf.at[3, rows_of(t)], hop_send.at[k, t], hop_recv.at[2, t], dev)

    lend = send(q.at[:, pl.ds(0, LENT), :], q.at[:, borrowed, :], lend_sem.at[0], lend_sem.at[1], ynb)
    give_back = send(lent, lent, lend_sem.at[2], lend_sem.at[3], ynb)

    n_key = WINDOW + TILE

    def nth(it):
        return jnp.where(it < 2, N_TILE - 1 - it, it - 2)

    def layer_tile(it, carry):
        t = nth(it)
        before = nth(jnp.maximum(it - 1, 0))
        rows = rows_of(t)
        cos, sin = cos_sin(hi4_ref, lo4_ref, me * TOK + t * TILE, TILE)
        a = rms(x[rows, :].astype(F32), 1.0 + ng_ref[0, 0:1, :]).astype(BF16)

        if fast:
            qs = [head_rope(dot(a, wq[0, h]), g4q, cos, sin) for h in range(4)]
        on(jnp.logical_and(me > 0, it < 2), halo_copy(t), 'wait_recv')
        for n in (1, 0):
            on(jnp.logical_and(me > 0, it == 2), halo_copy(n), 'wait_recv')
        start = pl.multiple_of(t * TILE, TILE)
        ks = win[pl.ds(start, n_key), 0:HEAD]
        vs = win[pl.ds(start, n_key), HEAD:2 * HEAD]
        col = lax.broadcasted_iota(jnp.int32, (1, n_key), 1)
        hidden = jnp.logical_and(me == 0, col + start < WINDOW)
        bias = jnp.where(hidden, NEG, -sigma if fast else 0.0)
        r = lax.broadcasted_iota(jnp.int32, (TILE, TILE), 0)
        c = lax.broadcasted_iota(jnp.int32, (TILE, TILE), 1)

        def local(h, q_h):
            s = dot_t(q_h, ks) * COEF + bias
            s = jnp.concatenate([jnp.where(c > r, s[:, 0:TILE], NEG), s[:, TILE:WINDOW], jnp.where(c <= r, s[:, WINDOW:], NEG)], axis=1)
            if not fast:
                s = s - jnp.max(s, axis=1, keepdims=True)
            p = jnp.exp2(s)
            total = jnp.sum(p, axis=1, keepdims=True)
            return dot(p.astype(BF16), vs) / total

        if fast:
            outs = [local(h, qs[h]).astype(BF16) for h in range(4)]
        else:
            def one(h, carry):
                acc[h, 0:TILE, :] = local(h, head_rope(dot(a, wq[0, h]), g4q, cos, sin))
                return carry
            heads(one)
            outs = [acc[h, 0:TILE, :].astype(BF16) for h in range(4)]
        h_mid = finish_rows(fast, x[rows, :], jnp.concatenate(outs, axis=1), ng_ref[0], wo, wg, wu, wd)
        mid[rows, :] = h_mid
        cos, sin = cos_sin(hi5_ref, lo5_ref, me * TOK + t * TILE, TILE)
        a = rms(h_mid.astype(F32), 1.0 + ng_ref[1, 0:1, :]).astype(BF16)
        kv5[rows, 0:HEAD] = head_rope(dot(a, wk[1]), g5k, cos, sin)
        kv5[rows, HEAD:2 * HEAD] = dot(a, wv[1]).astype(BF16)

        def project(h, carry):
            q[h, rows, :] = head_rope(dot(a, wq[1, h]), g5q, cos, sin)
            return carry

        heads(project)
        for cond, cp in hops(t):
            on(cond, cp, 'start')
        on(jnp.logical_and(far, it == 2), lend, 'start')

        @pl.when(jnp.logical_and(far, it >= 1))
        def _():
            first_in(before)
            early_pass(before).start()

        @pl.when(jnp.logical_and(me == 6, it >= 1))
        def _():
            third_in(before)
            over_pass(1, before, ynb).start()
        return carry

    lax.fori_loop(0, N_TILE, layer_tile, 0)
    outs5 = [pltpu.make_async_copy(kv5.at[:, pl.ds(0, HEAD)], k_hbm, out_sem.at[0]), pltpu.make_async_copy(kv5.at[:, pl.ds(HEAD, HEAD)], v_hbm, out_sem.at[1])]
    for cp in outs5 + ff5:
        cp.start()

    def attend(ks, vs, rows, width, masked, first, shift=None):
        n = rows.size
        if masked:
            r = lax.broadcasted_iota(jnp.int32, (n, n), 0)
            vis = lax.broadcasted_iota(jnp.int32, (n, n), 1) <= r
        if shift is not None:
            r = lax.broadcasted_iota(jnp.int32, (n, width), 0) + shift
            vis = lax.broadcasted_iota(jnp.int32, (n, width), 1) <= r
        def one(h, carry):
            s = dot_t(q[h, rows, :], ks)
            t = s * COEF - sigma if fast else s * COEF
            if shift is not None:
                t = jnp.where(vis, t, NEG)
            if masked:
                tail = jnp.where(vis, t[:, width - n:], NEG)
                t = tail if width == n else jnp.concatenate([t[:, 0:width - n], tail], axis=1)
            if not fast:
                mx = jnp.broadcast_to(jnp.max(t, axis=1, keepdims=True), (n, 128))
                fresh = mx if first else jnp.maximum(m[h, rows, :], mx)
                if not first:
                    decay = jnp.exp2(m[h, rows, :] - fresh)
                    l[h, rows, :] = l[h, rows, :] * decay
                    acc[h, rows, :] = acc[h, rows, :] * decay[:, 0:1]
                m[h, rows, :] = fresh
                t = t - fresh[:, 0:1]
            p = jnp.exp2(t)
            lp = p[:, 0:128]
            for j in range(1, width // 128):
                lp = lp + p[:, j * 128:(j + 1) * 128]
            o = dot(p.astype(BF16), vs)
            if first:
                l[h, rows, :] = lp
                acc[h, rows, :] = o
            else:
                l[h, rows, :] += lp
                acc[h, rows, :] += o
            return carry

        heads(one)

    base = jnp.where(far, LENT // TILE, 0)
    if not fast:
        def diag(i, carry):
            attend(kv5[:, 0:HEAD], kv5[:, HEAD:2 * HEAD], rows_of(i), TOK, False, True, i * TILE)
            return carry
        lax.fori_loop(base, N_TILE, diag, 0)
    for i in range(N_TILE if fast else 0):
        width = (i + 1) * TILE

        @pl.when(jnp.logical_or(i > 0, jnp.logical_not(far)))
        def _(i=i, width=width):
            attend(kv5[0:width, 0:HEAD], kv5[0:width, HEAD:2 * HEAD], pl.ds(i * TILE, TILE), width, True, True)

    def slot(s):
        ks = buf[s, :, 0:HEAD]
        vs = buf[s, :, HEAD:2 * HEAD]

        def q_rows(n, base):
            def one(i, carry):
                attend(ks, vs, pl.ds(pl.multiple_of(base + i * n, 128), n), TOK, False, False)
                return carry
            lax.fori_loop(0, (TOK - base) // n, one, 0)

        if not fast:
            def one(i, carry):
                attend(ks, vs, rows_of(i), TOK, False, False)
                return carry
            lax.fori_loop(base, N_TILE, one, 0)
            return

        @pl.when(far)
        def _():
            q_rows((TOK - LENT) // 2, LENT)

        @pl.when(jnp.logical_not(far))
        def _():
            q_rows(QROWS, 0)

    def wide(s, dst, ssem, dev):
        return send(buf.at[s], buf.at[dst], ssem, wide_recv.at[dst], dev)

    def relay(s):
        odd = s % 2 == 1
        return [(odd, wide(s, jnp.minimum(s + 1, N_SLOT - 1), pass_send.at[s], partner)),
                (jnp.logical_and(jnp.logical_and(chip == 1, core == 0), s == 1), wide(s, 5, over_send, ynb)),
                (jnp.logical_and(jnp.logical_and(chip == 2, core == 1), s == 1), wide(s, 5, over_send, xnb))]

    def chunks_in(cond, slot_no, rk, n=N_TILE):
        @pl.when(cond)
        def _():
            def one(t, carry):
                send(kv5.at[rows_of(t)], buf.at[slot_no, rows_of(t)], hop_send.at[0, t], hop_recv.at[rk, t], partner).wait_recv()
                return carry
            lax.fori_loop(0, n, one, 0)

    gives = jnp.logical_or(me == 3, jnp.logical_or(me == 5, me == 1))
    spread = [(gives, send(last, last, last_send.at[0], last_recv, partner)), (me == 3, send(last, last, last_send.at[1], last_recv, xnb))]

    def pass_last(cond):
        @pl.when(cond)
        def _():
            send(last, last, last_send.at[2], last_recv, partner).wait_recv()
            for c, cp in spread:
                on(c, cp, 'start')

    pass_last(jnp.logical_and(gives, me > 1))

    def step(s, carry):
        chunks_in(jnp.logical_and(s == 0, core == 1), 0, 0)
        chunks_in(jnp.logical_and(s == 1, chip < 3), 1, 1)
        chunks_in(jnp.logical_and(s == 3, me != 6), 3, 2)

        @pl.when(jnp.logical_and(far, jnp.where(core == 1, s == 0, s == 1)))
        def _():
            first_in(1)
            early_pass(1).start()

        @pl.when(jnp.logical_and(me == 6, s == 1))
        def _():
            third_in(1)
            over_pass(1, 1, ynb).start()

        @pl.when(jnp.logical_or(jnp.logical_and(s > 0, s % 2 == 0), s == 5))
        def _():
            wide(s, s, pass_send.at[s], partner).wait_recv()

        for cond, cp in relay(s):
            on(cond, cp, 'start')

        @pl.when(jnp.logical_or(s >= 1, core == 1))
        def _():
            slot(s)

        return carry

    @pl.when(me == 1)
    def _():
        def one(it, carry):
            t = nth(it)
            third_in(t)
            over_pass(3, t, xnb).start()
            return carry
        lax.fori_loop(0, N_TILE, one, 0)

    lax.fori_loop(0, 2 * chip + 1, step, 0)
    pass_last(me == 1)

    pass_six = send(buf.at[5], buf.at[5], pass_send.at[5], wide_recv.at[5], partner)
    pass_three = send(buf.at[3], buf.at[4], pass_send.at[3], wide_recv.at[4], partner)
    gets_six = jnp.logical_and(helper, core == 0)

    @pl.when(helper)
    def _():
        chunks_in(core == 0, 5, 3)
        chunks_in(core == 1, 6, 3, 1)
        on(core == 0, pass_six, 'start')
        chunks_in(core == 1, 3, 2)
        on(core == 1, pass_three, 'start')
        lend.wait_recv()
        attend(buf[5 + core, 0:LENT, 0:HEAD], buf[5 + core, 0:LENT, HEAD:2 * HEAD], borrowed, LENT, True, True)

        def block(k, carry):
            s = jnp.where(k == 0, OWN, jnp.where(k <= 4, k - 1, jnp.where(k == 5, 5, 4)))
            chunks_in(jnp.logical_and(k == 1, core == 0), 0, 0)
            chunks_in(jnp.logical_and(k == 4, core == 0), 3, 2)
            on(jnp.logical_and(k == 4, core == 0), pass_three, 'start')
            on(jnp.logical_and(k == 5, core == 1), pass_six, 'wait_recv')
            on(k == 6, pass_three, 'wait_recv')

            @pl.when(jnp.logical_or(k != 5, core == 1))
            def _():
                attend(buf[s, :, 0:HEAD], buf[s, :, HEAD:2 * HEAD], borrowed, TOK, False, False)
            return carry

        lax.fori_loop(0, 7, block, 0)
        for h in range(4):
            total = jnp.sum(l[h, borrowed, :], axis=1, keepdims=True)
            lent[h] = (acc[h, borrowed, :] / total).astype(BF16)
        give_back.start()

    @pl.when(jnp.logical_and(jnp.logical_not(gives), jnp.logical_not(is_last)))
    def _():
        send(last, last, last_send.at[2], last_recv, partner).wait_recv()

    def put_last(src):
        return [pltpu.make_async_copy(src.at[:, pl.ds(0, HEAD)], kl_hbm, out_sem.at[2]), pltpu.make_async_copy(src.at[:, pl.ds(HEAD, HEAD)], vl_hbm, out_sem.at[3])]

    for cp in put_last(own4):
        on(is_last, cp, 'start')
    for cp in put_last(last):
        on(jnp.logical_not(is_last), cp, 'start')

    for cp in ff5:
        cp.wait()

    def out_copy(t):
        return pltpu.make_async_copy(xo.at[rows_of(t, FROWS)], out_hbm.at[rows_of(t, FROWS)], out_sem.at[4 + t])

    def finish_tile(it, carry):
        t = (it + 1) % (TOK // FROWS)

        @pl.when(jnp.logical_and(far, t == 0))
        def _():
            give_back.wait_recv()
            for h in range(4):
                acc[h, 0:LENT, :] = lent[h].astype(F32)
                l[h, 0:LENT, :] = jnp.full((LENT, 128), 1.0 / 128.0, F32)

        rows = rows_of(t, FROWS)
        attn = []
        for h in range(4):
            total = jnp.sum(l[h, rows, :], axis=1, keepdims=True)
            attn.append((acc[h, rows, :] / total).astype(BF16))
        xo[rows, :] = finish_rows(fast, mid[rows, :], jnp.concatenate(attn, axis=1), ng_ref[1], wo, wg, wu, wd)
        out_copy(t).start()
        return carry

    lax.fori_loop(0, TOK // FROWS, finish_tile, 0)

    def drain_tile(t, carry):
        on(me < top, halo_copy(t), 'wait_send')
        on(far, early_pass(t), 'wait_send')
        on(me == 1, over_pass(3, t, xnb), 'wait_send')
        on(me == 6, over_pass(1, t, ynb), 'wait_send')
        for cond, cp in hops(t):
            on(cond, cp, 'wait_send')
        return carry

    lax.fori_loop(0, N_TILE, drain_tile, 0)

    def drain_step(s, carry):
        for cond, cp in relay(s):
            on(cond, cp, 'wait_send')
        return carry

    lax.fori_loop(1, 2 * chip + 1, drain_step, 0)
    for cp in last_cps:
        on(is_last, cp, 'wait_send')
    on(far, lend, 'wait_send')
    on(helper, give_back, 'wait_send')
    on(helper, pass_three, 'wait_send')
    on(gets_six, pass_six, 'wait_send')
    for cond, cp in spread:
        on(cond, cp, 'wait_send')
    for cp in outs5 + put_last(last):
        cp.wait()
    for t in range(TOK // FROWS):
        out_copy(t).wait()


def layers(fast, ng, qg, rope, x, wq, wk, wv, wo, wg, wu, wd):
    vm = pl.BlockSpec(memory_space=pltpu.VMEM)
    anyw = pl.BlockSpec(memory_space=pl.ANY)
    dma = pltpu.SemaphoreType.DMA
    kshape = jax.ShapeDtypeStruct((TOK, HEAD), BF16)
    return pl.pallas_call(
        functools.partial(layers_kernel, fast),
        in_specs=[vm] * 6 + [anyw] * 8,
        out_specs=[anyw] * 5 + [pl.BlockSpec(memory_space=pltpu.SMEM)],
        out_shape=[jax.ShapeDtypeStruct((TOK, D), BF16), kshape, kshape, kshape, kshape, jax.ShapeDtypeStruct((1,), F32)],
        scratch_shapes=[
            pltpu.VMEM((TOK, D), BF16), pltpu.VMEM((TOK, D), BF16), pltpu.VMEM((WINDOW + TOK, 2 * HEAD), BF16),
            pltpu.VMEM((4, TOK + LENT, HEAD), BF16), pltpu.VMEM((N_SLOT, TOK, 2 * HEAD), BF16), pltpu.VMEM((4, TOK + LENT, HEAD), F32),
            pltpu.VMEM((4, TOK + LENT, 128), F32), pltpu.VMEM((8, 128) if fast else (4, TOK + LENT, 128), F32),
            pltpu.VMEM((4, LENT, HEAD), BF16), pltpu.VMEM((TOK, 2 * HEAD), BF16), pltpu.VMEM((TOK, D), BF16),
            pltpu.VMEM((2, 4, D, HEAD), BF16), pltpu.VMEM((2, D, HEAD), BF16), pltpu.VMEM((2, D, HEAD), BF16),
            pltpu.VMEM((4 * HEAD, D), BF16), pltpu.VMEM((D, FF), BF16), pltpu.VMEM((D, FF), BF16), pltpu.VMEM((FF, D), BF16),
            dma((11,)), dma((4 + TOK // FROWS,)), dma((N_TILE,)), dma((N_TILE,)), dma((4, N_TILE)), dma((4, N_TILE)), dma((N_SLOT,)), dma, dma((N_SLOT,)),
            dma((3,)), dma, dma((4,))],
        name="layers_fast" if fast else "layers_safe",
        compiler_params=pltpu.CompilerParams(vmem_limit_bytes=VLIM, collective_id=0 if fast else None, has_side_effects=True),
        cost_estimate=pl.CostEstimate(flops=60 * 10**9, bytes_accessed=30 << 20, transcendentals=0),
    )(ng, qg, *rope[0], *rope[1], x, wq, wk, wv, wo, wg, wu, wd)


def emit_kernel(*refs):
    ins, outs, mids, sem_in, sem_out = refs[0:5], refs[5:10], refs[10:15], refs[15], refs[16]
    loads = [pltpu.make_async_copy(i, m, sem_in.at[n]) for n, (i, m) in enumerate(zip(ins, mids))]
    stores = [pltpu.make_async_copy(m, o, sem_out.at[n]) for n, (m, o) in enumerate(zip(mids, outs))]
    for cp in loads:
        cp.start()
    for ld, st in zip(loads, stores):
        ld.wait()
        st.start()
    for st in stores:
        st.wait()


def emit(arrays):
    anyw = pl.BlockSpec(memory_space=pl.ANY)
    return pl.pallas_call(
        emit_kernel,
        in_specs=[anyw] * 5,
        out_specs=[anyw] * 5,
        out_shape=[jax.ShapeDtypeStruct(a.shape, a.dtype) for a in arrays],
        scratch_shapes=[pltpu.VMEM(a.shape, a.dtype) for a in arrays] + [pltpu.SemaphoreType.DMA((5,)), pltpu.SemaphoreType.DMA((5,))],
        name="emit",
    )(*arrays)


def solution(mesh):
    n_dev = mesh.shape['cp']
    rope = [rope_const(layer, TOK * n_dev) for layer in range(2)]

    def shard_body(x, ng, qg, w_q, w_k, w_v, w_o, w_gate, w_up, w_down):
        wq = w_q.transpose(0, 2, 1, 3)
        wk = w_k.reshape(2, D, HEAD)
        wv = w_v.reshape(2, D, HEAD)
        wo = w_o.reshape(2, 4 * HEAD, D)

        def run(fast):
            return tuple(layers(fast, ng, qg, rope, x, wq, wk, wv, wo, w_gate, w_up, w_down))

        *first, bound = run(True)
        _, rest = lax.while_loop(lambda c: c[0], lambda c: (jnp.zeros((), jnp.bool_), run(False)[:5]), (bound[0] > LIMIT, tuple(first)))
        out, k5, v5, kl, vl = emit(rest)
        return out, k5[:, None, :], v5[:, None, :], kl[:, None, :], vl[:, None, :]

    return jax.shard_map(shard_body, mesh=mesh, in_specs=(P('cp'), P(), P(), P(), P(), P(), P(), P(), P(), P()),
                         out_specs=(P('cp'), P('cp'), P('cp'), P(), P()), check_vma=False)
```

profile of v0, /device:TPU:7, one launch (start us, length us, event | category | flops | bytes accessed | tf_op | source)
XLA Modules:
  0.0 91.8 jit_solution(15426077133739603778)
XLA Ops:
  0.6 0.0 copy-start
  0.6 0.0 copy-start.2
  0.7 0.0 copy-start.3
  0.7 0.0 copy-start.4
  0.7 2.2 %copy.21 = bf16[2,640,4,256]{3,1,2,0:T(8,128)(2,1)S(1)} copy(bf16[2,640,4,256]{3,2,1,0:T(4,128)(2,1)} %param.19) | data formatting | bytes 5242880 | tf_op args[3]
  2.9 0.2 copy-done
  3.2 0.1 copy-done.2
  3.3 0.0 copy-done.3
  3.3 0.0 copy-done.4
  3.3 84.3 %layers_fast.1 = (bf16[1024,640]{1,0:T(8,128)(2,1)}, bf16[1024,256]{1,0:T(8,128)(2,1)}, bf16[1024,256]{1,0:T(8,128)(2,1)}, bf16[1024,256]{1,0:T(8,128)(2,1)}, bf16[1024,256]{1,0:T(8,128)(2,1)}, /*index=5*/f32[1]{0:T(128)}) custom-call(f32[2,4,640]{2,1,0:T(4,128)S(1)} %copy-done.3, f32[2,2,256]{2,1,0:T(2,128)S(1)} %copy-done.4, ...), custom_call_target="tpu_custom_call" | custom-call | flops 60000002048 | bytes 31457280 | tf_op jit(solution)/shard_map/layers_fast/pallas_call | solution.py:545
  88.2 0.2 while.18
  88.5 3.1 %emit.1 = (bf16[1024,640]{1,0:T(8,128)(2,1)}, bf16[1024,256]{1,0:T(8,128)(2,1)}, bf16[1024,256]{1,0:T(8,128)(2,1)}, bf16[1024,256]{1,0:T(8,128)(2,1)}, bf16[1024,256]{1,0:T(8,128)(2,1)}) custom-call(bf16[1024,640]{1,0:T(8,128)(2,1)} %get-tuple-element.289, bf16[1024,256]{1,0:T(8,128)(2,1)} %get-tuple-element.290, bf16[1024,256]{1,0:T(8,128)(2,1)} %get-tuple-element.291, ...), custom_call_target="tpu_custom_call" | custom-call | tf_op jit(solution)/shard_map/emit/pallas_call | solution.py:580
Async XLA Ops:
  0.6 2.5 %copy-start = (bf16[2,4,256,640]{3,2,1,0:T(8,128)(2,1)S(1)}, bf16[2,4,256,640]{3,2,1,0:T(8,128)(2,1)}, u32[]{:S(2)}) copy-start(bf16[2,4,256,640]{3,2,1,0:T(8,128)(2,1)} %param.22) | copy-start | bytes 7864324
  0.6 2.7 %copy-start.2 = (bf16[2,640,1,256]{3,1,2,0:T(8,128)(2,1)S(1)}, bf16[2,640,1,256]{3,1,2,0:T(8,128)(2,1)}, u32[]{:S(2)}) copy-start(bf16[2,640,1,256]{3,1,2,0:T(8,128)(2,1)} %param.20) | copy-start | bytes 1966084
  0.7 2.6 %copy-start.3 = (f32[2,4,640]{2,1,0:T(4,128)S(1)}, f32[2,4,640]{2,1,0:T(4,128)}, u32[]{:S(2)}) copy-start(f32[2,4,640]{2,1,0:T(4,128)} %ng_ref.1) | copy-start | bytes 61444
  0.7 2.6 %copy-start.4 = (f32[2,2,256]{2,1,0:T(2,128)S(1)}, f32[2,2,256]{2,1,0:T(2,128)}, u32[]{:S(2)}) copy-start(f32[2,2,256]{2,1,0:T(2,128)} %qg_ref.1) | copy-start | bytes 12292
where the time goes:
time: 91.9 us; the launch traced here: 91.8 us
  Pallas kernels  87.5 us (95%)
  local copies, waits for them, and re-layouts  2.63 us (3%)
  between operations  1.44 us (2%)
    pallas_call x1, Pallas kernels, layers(): pl.pallas_call(functools.partial(layers_kernel, fast), in_specs=[vm] * 6...  84.3 us
    pallas_call x1, Pallas kernels, emit(): pl.pallas_call(emit_kernel, in_specs=[anyw] * 5, out_specs=[anyw] * 5, ou...  3.15 us
    unnamed x9, local copies, waits for them, and re-layouts  2.63 us

commit v1 on v0

--- a/solution.py
+++ b/solution.py
@@ -77,28 +77,34 @@
 N_TILE = TOK // TILE
 QROWS = 512
 FROWS = 512
+PARTS = 2
 
 
 def finish_rows(fast, x, attn, ng, wo, wg, wu, wd):
-    o = dot(attn, wo[...]).astype(BF16).astype(F32)
-    h1 = (x.astype(F32) + rms(o, 1.0 + ng[1:2, :])).astype(BF16)
-    b = rms(h1.astype(F32), 1.0 + ng[2:3, :]).astype(BF16)
-
-    def ff(cols):
+    n = PARTS if fast else 1
+    size = x.shape[0] // n
+    groups = [slice(i * size, (i + 1) * size) for i in range(n)]
+
+    def ff(b, cols):
         m = (jax.nn.gelu(dot(b, wg[:, cols]), approximate=True) * dot(b, wu[:, cols])).astype(BF16)
-        return dot(m, wd[cols, :])
-
+        return m if fast else dot(m, wd[cols, :])
+
+    o = [dot(attn[g], wo[...]).astype(BF16).astype(F32) for g in groups]
+    h1, b = [], []
+    for g, o_g in zip(groups, o):
+        h1.append((x[g].astype(F32) + rms(o_g, 1.0 + ng[1:2, :])).astype(BF16))
+        b.append(rms(h1[-1].astype(F32), 1.0 + ng[2:3, :]).astype(BF16))
     if fast:
-        acc = ff(slice(None))
+        m = [ff(b_g, slice(None)) for b_g in b]
+        y = [dot(m_g, wd[...]) for m_g in m]
     else:
-        acc = lax.fori_loop(0, FF // 256, lambda f, part: part + ff(pl.ds(pl.multiple_of(f * 256, 256), 256)), jnp.zeros(h1.shape, F32))
-    o2 = acc.astype(BF16).astype(F32)
-    return (h1.astype(F32) + rms(o2, 1.0 + ng[3:4, :])).astype(BF16)
-
-
-def layers_kernel(fast, ng_ref, qg_ref, hi4_ref, lo4_ref, hi5_ref, lo5_ref, x_hbm, wq_hbm, wk_hbm, wv_hbm, wo_hbm, wg_hbm, wu_hbm, wd_hbm,
+        y = [lax.fori_loop(0, FF // 256, lambda f, part: part + ff(b[0], pl.ds(pl.multiple_of(f * 256, 256), 256)), jnp.zeros(x.shape, F32))]
+    return [(h_g.astype(F32) + rms(y_g.astype(BF16).astype(F32), 1.0 + ng[3:4, :])).astype(BF16) for h_g, y_g in zip(h1, y)]
+
+
+def layers_kernel(fast, ng_hbm, qg_hbm, hi4_hbm, lo4_hbm, hi5_hbm, lo5_hbm, x_hbm, wq_hbm, wk_hbm, wv_hbm, wo_hbm, wg_hbm, wu_hbm, wd_hbm,
                   out_hbm, k_hbm, v_hbm, kl_hbm, vl_hbm, bound_ref,
-                  x, mid, win, q, buf, acc, l, m, lent, last, xo, wq, wk, wv, wo, wg, wu, wd,
+                  ng_ref, qg_ref, hi4_ref, lo4_ref, hi5_ref, lo5_ref, x, mid, win, q, buf, acc, l, m, lent, last, xo, wq, wk, wv, wo, wg, wu, wd,
                   load_sem, out_sem, halo_send, halo_recv, hop_send, hop_recv, pass_send, over_send, wide_recv, last_send, last_recv, lend_sem):
     me = lax.axis_index('cp')
     core = me % 2
@@ -115,11 +121,14 @@
     def load(src, dst, n):
         return pltpu.make_async_copy(src, dst, load_sem.at[n])
 
+    turns = pl.ds(pl.multiple_of(me * (TOK // LO), TOK // LO), TOK // LO)
+    small = [load(ng_hbm, ng_ref, 11), load(qg_hbm, qg_ref, 12), load(hi4_hbm.at[turns], hi4_ref, 13), load(lo4_hbm, lo4_ref, 14),
+             load(hi5_hbm.at[turns], hi5_ref, 15), load(lo5_hbm, lo5_ref, 16)]
     early = [load(x_hbm, x, 0), load(wk_hbm.at[0], wk.at[0], 1), load(wv_hbm.at[0], wv.at[0], 2), load(wq_hbm.at[0], wq.at[0], 3)]
     ff4 = [load(wo_hbm.at[0], wo, 4), load(wg_hbm.at[0], wg, 5), load(wu_hbm.at[0], wu, 6), load(wd_hbm.at[0], wd, 7)]
     next_qkv = [load(wk_hbm.at[1], wk.at[1], 8), load(wv_hbm.at[1], wv.at[1], 9), load(wq_hbm.at[1], wq.at[1], 10)]
     ff5 = [load(wo_hbm.at[1], wo, 4), load(wg_hbm.at[1], wg, 5), load(wu_hbm.at[1], wu, 6), load(wd_hbm.at[1], wd, 7)]
-    for cp in early:
+    for cp in small + early:
         cp.start()
 
     if fast:
@@ -133,8 +142,6 @@
     def _():
         win[0:WINDOW, :] = jnp.zeros((WINDOW, 2 * HEAD), BF16)
 
-    if fast:
-        pl.semaphore_wait(barrier, 5)
 
     def send(src, dst, ssem, rsem, dev):
         return pltpu.make_async_remote_copy(src_ref=src, dst_ref=dst, send_sem=ssem, recv_sem=rsem, device_id=(dev,), device_id_type=MESH)
@@ -157,6 +164,8 @@
     def halo_copy(t):
         return send(win.at[rows_of(t + N_TILE)], win.at[rows_of(t)], halo_send.at[t], halo_recv.at[t], (me + 1) % 8)
 
+    for cp in small + early[:3]:
+        cp.wait()
     gains = jnp.abs(1.0 + qg_ref[...])
     pair = jnp.maximum(gains[:, :, 0:HEAD // 2], gains[:, :, HEAD // 2:])
     bound = 16.0 * 1.02 * jnp.max(pair[:, 0:1] * pair[:, 1:2])
@@ -164,15 +173,17 @@
     sigma = jnp.maximum(bound - TOP, 0.0) * LOG2E
     g4q, g4k = 1.0 + qg_ref[0, 0:1, :], 1.0 + qg_ref[0, 1:2, :]
     g5q, g5k = 1.0 + qg_ref[1, 0:1, :], 1.0 + qg_ref[1, 1:2, :]
-    for cp in early[:3]:
-        cp.wait()
-
     def kv_tile(it, carry):
         t = N_TILE - 1 - it
-        cos, sin = cos_sin(hi4_ref, lo4_ref, me * TOK + t * TILE, TILE)
+        cos, sin = cos_sin(hi4_ref, lo4_ref, t * TILE, TILE)
         a = rms(x[rows_of(t), :].astype(F32), 1.0 + ng_ref[0, 0:1, :]).astype(BF16)
+        mid[rows_of(t), :] = a
         win[rows_of(t + N_TILE), 0:HEAD] = head_rope(dot(a, wk[0]), g4k, cos, sin)
         win[rows_of(t + N_TILE), HEAD:2 * HEAD] = dot(a, wv[0]).astype(BF16)
+        if fast:
+            @pl.when(it == 0)
+            def _():
+                pl.semaphore_wait(barrier, 5)
         on(me < top, halo_copy(t), 'start')
         return carry
 
@@ -221,8 +232,8 @@
         t = nth(it)
         before = nth(jnp.maximum(it - 1, 0))
         rows = rows_of(t)
-        cos, sin = cos_sin(hi4_ref, lo4_ref, me * TOK + t * TILE, TILE)
-        a = rms(x[rows, :].astype(F32), 1.0 + ng_ref[0, 0:1, :]).astype(BF16)
+        cos, sin = cos_sin(hi4_ref, lo4_ref, t * TILE, TILE)
+        a = mid[rows, :]
 
         if fast:
             qs = [head_rope(dot(a, wq[0, h]), g4q, cos, sin) for h in range(4)]
@@ -256,14 +267,20 @@
             heads(one)
             outs = [acc[h, 0:TILE, :].astype(BF16) for h in range(4)]
         h_mid = finish_rows(fast, x[rows, :], jnp.concatenate(outs, axis=1), ng_ref[0], wo, wg, wu, wd)
-        mid[rows, :] = h_mid
-        cos, sin = cos_sin(hi5_ref, lo5_ref, me * TOK + t * TILE, TILE)
-        a = rms(h_mid.astype(F32), 1.0 + ng_ref[1, 0:1, :]).astype(BF16)
-        kv5[rows, 0:HEAD] = head_rope(dot(a, wk[1]), g5k, cos, sin)
-        kv5[rows, HEAD:2 * HEAD] = dot(a, wv[1]).astype(BF16)
+        cos, sin = cos_sin(hi5_ref, lo5_ref, t * TILE, TILE)
+        size = TILE // len(h_mid)
+        parts = []
+        for i, h_g in enumerate(h_mid):
+            here = pl.ds(pl.multiple_of(t * TILE + i * size, size), size)
+            mid[here, :] = h_g
+            parts.append((here, rms(h_g.astype(F32), 1.0 + ng_ref[1, 0:1, :]).astype(BF16), cos[i * size:(i + 1) * size], sin[i * size:(i + 1) * size]))
+        for here, a_g, cos_g, sin_g in parts:
+            kv5[here, 0:HEAD] = head_rope(dot(a_g, wk[1]), g5k, cos_g, sin_g)
+            kv5[here, HEAD:2 * HEAD] = dot(a_g, wv[1]).astype(BF16)
 
         def project(h, carry):
-            q[h, rows, :] = head_rope(dot(a, wq[1, h]), g5q, cos, sin)
+            for here, a_g, cos_g, sin_g in parts:
+                q[h, here, :] = head_rope(dot(a_g, wq[1, h]), g5q, cos_g, sin_g)
             return carry
 
         heads(project)
@@ -359,7 +376,7 @@
 
         @pl.when(far)
         def _():
-            q_rows((TOK - LENT) // 2, LENT)
+            q_rows(TOK - LENT, LENT)
 
         @pl.when(jnp.logical_not(far))
         def _():
@@ -500,7 +517,7 @@
         for h in range(4):
             total = jnp.sum(l[h, rows, :], axis=1, keepdims=True)
             attn.append((acc[h, rows, :] / total).astype(BF16))
-        xo[rows, :] = finish_rows(fast, mid[rows, :], jnp.concatenate(attn, axis=1), ng_ref[1], wo, wg, wu, wd)
+        xo[rows, :] = jnp.concatenate(finish_rows(fast, mid[rows, :], jnp.concatenate(attn, axis=1), ng_ref[1], wo, wg, wu, wd), axis=0)
         out_copy(t).start()
         return carry
 
@@ -538,23 +555,23 @@
 
 
 def layers(fast, ng, qg, rope, x, wq, wk, wv, wo, wg, wu, wd):
-    vm = pl.BlockSpec(memory_space=pltpu.VMEM)
     anyw = pl.BlockSpec(memory_space=pl.ANY)
     dma = pltpu.SemaphoreType.DMA
     kshape = jax.ShapeDtypeStruct((TOK, HEAD), BF16)
     return pl.pallas_call(
         functools.partial(layers_kernel, fast),
-        in_specs=[vm] * 6 + [anyw] * 8,
+        in_specs=[anyw] * 14,
         out_specs=[anyw] * 5 + [pl.BlockSpec(memory_space=pltpu.SMEM)],
         out_shape=[jax.ShapeDtypeStruct((TOK, D), BF16), kshape, kshape, kshape, kshape, jax.ShapeDtypeStruct((1,), F32)],
         scratch_shapes=[
-            pltpu.VMEM((TOK, D), BF16), pltpu.VMEM((TOK, D), BF16), pltpu.VMEM((WINDOW + TOK, 2 * HEAD), BF16),
+            pltpu.VMEM((2, 4, D), F32), pltpu.VMEM((2, 2, HEAD), F32), pltpu.VMEM((TOK // LO, HEAD), F32), pltpu.VMEM((LO, HEAD), F32),
+            pltpu.VMEM((TOK // LO, HEAD), F32), pltpu.VMEM((LO, HEAD), F32), pltpu.VMEM((TOK, D), BF16), pltpu.VMEM((TOK, D), BF16), pltpu.VMEM((WINDOW + TOK, 2 * HEAD), BF16),
             pltpu.VMEM((4, TOK + LENT, HEAD), BF16), pltpu.VMEM((N_SLOT, TOK, 2 * HEAD), BF16), pltpu.VMEM((4, TOK + LENT, HEAD), F32),
             pltpu.VMEM((4, TOK + LENT, 128), F32), pltpu.VMEM((8, 128) if fast else (4, TOK + LENT, 128), F32),
             pltpu.VMEM((4, LENT, HEAD), BF16), pltpu.VMEM((TOK, 2 * HEAD), BF16), pltpu.VMEM((TOK, D), BF16),
             pltpu.VMEM((2, 4, D, HEAD), BF16), pltpu.VMEM((2, D, HEAD), BF16), pltpu.VMEM((2, D, HEAD), BF16),
             pltpu.VMEM((4 * HEAD, D), BF16), pltpu.VMEM((D, FF), BF16), pltpu.VMEM((D, FF), BF16), pltpu.VMEM((FF, D), BF16),
-            dma((11,)), dma((4 + TOK // FROWS,)), dma((N_TILE,)), dma((N_TILE,)), dma((4, N_TILE)), dma((4, N_TILE)), dma((N_SLOT,)), dma, dma((N_SLOT,)),
+            dma((17,)), dma((4 + TOK // FROWS,)), dma((N_TILE,)), dma((N_TILE,)), dma((4, N_TILE)), dma((4, N_TILE)), dma((N_SLOT,)), dma, dma((N_SLOT,)),
             dma((3,)), dma, dma((4,))],
         name="layers_fast" if fast else "layers_safe",
         compiler_params=pltpu.CompilerParams(vmem_limit_bytes=VLIM, collective_id=0 if fast else None, has_side_effects=True),

time: 91.9 us -> 89.5 us (0.974)
  Pallas kernels: 87.5 us -> 85.1 us
    pallas_call x1, Pallas kernels: 84.3 us -> 81.9 us  [layers(): pl.pallas_call(functools.partial(layers_kernel, fast), in_specs=[anyw] *...]
where the time goes in v1:
time: 89.5 us; the launch traced here: 89.4 us
  Pallas kernels  85.1 us (95%)
  local copies, waits for them, and re-layouts  2.63 us (3%)
  between operations  1.44 us (2%)
    pallas_call x1, Pallas kernels, layers(): pl.pallas_call(functools.partial(layers_kernel, fast), in_specs=[anyw] *...  81.9 us
    pallas_call x1, Pallas kernels, emit(): pl.pallas_call(emit_kernel, in_specs=[anyw] * 5, out_specs=[anyw] * 5, ou...  3.15 us
    unnamed x9, local copies, waits for them, and re-layouts  2.63 us

profile of v1, /device:TPU:7, one launch (start us, length us, event | category | flops | bytes accessed | tf_op | source)
XLA Modules:
  0.0 89.4 jit_solution(16443521386953660865)
XLA Ops:
  0.6 0.0 copy-start
  0.6 0.0 copy-start.2
  0.7 0.0 copy-start.3
  0.7 0.0 copy-start.4
  0.7 2.2 %copy.21 = bf16[2,640,4,256]{3,1,2,0:T(8,128)(2,1)S(1)} copy(bf16[2,640,4,256]{3,2,1,0:T(4,128)(2,1)} %param.19) | data formatting | bytes 5242880 | tf_op args[3]
  2.9 0.2 copy-done
  3.2 0.1 copy-done.2
  3.3 0.0 copy-done.3
  3.3 0.0 copy-done.4
  3.3 81.9 %layers_fast.1 = (bf16[1024,640]{1,0:T(8,128)(2,1)}, bf16[1024,256]{1,0:T(8,128)(2,1)}, bf16[1024,256]{1,0:T(8,128)(2,1)}, bf16[1024,256]{1,0:T(8,128)(2,1)}, bf16[1024,256]{1,0:T(8,128)(2,1)}, /*index=5*/f32[1]{0:T(128)}) custom-call(f32[2,4,640]{2,1,0:T(4,128)S(1)} %copy-done.3, f32[2,2,256]{2,1,0:T(2,128)S(1)} %copy-done.4, ...), custom_call_target="tpu_custom_call" | custom-call | flops 60000002048 | bytes 31457280 | tf_op jit(solution)/shard_map/layers_fast/pallas_call | solution.py:561
  85.8 0.2 while.18
  86.0 3.1 %emit.1 = (bf16[1024,640]{1,0:T(8,128)(2,1)}, bf16[1024,256]{1,0:T(8,128)(2,1)}, bf16[1024,256]{1,0:T(8,128)(2,1)}, bf16[1024,256]{1,0:T(8,128)(2,1)}, bf16[1024,256]{1,0:T(8,128)(2,1)}) custom-call(bf16[1024,640]{1,0:T(8,128)(2,1)} %get-tuple-element.289, bf16[1024,256]{1,0:T(8,128)(2,1)} %get-tuple-element.290, bf16[1024,256]{1,0:T(8,128)(2,1)} %get-tuple-element.291, ...), custom_call_target="tpu_custom_call" | custom-call | tf_op jit(solution)/shard_map/emit/pallas_call | solution.py:597
Async XLA Ops:
  0.6 2.5 %copy-start = (bf16[2,4,256,640]{3,2,1,0:T(8,128)(2,1)S(1)}, bf16[2,4,256,640]{3,2,1,0:T(8,128)(2,1)}, u32[]{:S(2)}) copy-start(bf16[2,4,256,640]{3,2,1,0:T(8,128)(2,1)} %param.22) | copy-start | bytes 7864324
  0.6 2.7 %copy-start.2 = (bf16[2,640,1,256]{3,1,2,0:T(8,128)(2,1)S(1)}, bf16[2,640,1,256]{3,1,2,0:T(8,128)(2,1)}, u32[]{:S(2)}) copy-start(bf16[2,640,1,256]{3,1,2,0:T(8,128)(2,1)} %param.20) | copy-start | bytes 1966084
  0.7 2.6 %copy-start.3 = (f32[2,4,640]{2,1,0:T(4,128)S(1)}, f32[2,4,640]{2,1,0:T(4,128)}, u32[]{:S(2)}) copy-start(f32[2,4,640]{2,1,0:T(4,128)} %ng_hbm.1) | copy-start | bytes 61444
  0.7 2.6 %copy-start.4 = (f32[2,2,256]{2,1,0:T(2,128)S(1)}, f32[2,2,256]{2,1,0:T(2,128)}, u32[]{:S(2)}) copy-start(f32[2,2,256]{2,1,0:T(2,128)} %qg_hbm.1) | copy-start | bytes 12292

commit v2 on v1

--- a/solution.py
+++ b/solution.py
@@ -391,13 +391,13 @@
                 (jnp.logical_and(jnp.logical_and(chip == 1, core == 0), s == 1), wide(s, 5, over_send, ynb)),
                 (jnp.logical_and(jnp.logical_and(chip == 2, core == 1), s == 1), wide(s, 5, over_send, xnb))]
 
-    def chunks_in(cond, slot_no, rk, n=N_TILE):
+    def chunks_in(cond, slot_no, rk, start=0, stop=N_TILE):
         @pl.when(cond)
         def _():
             def one(t, carry):
                 send(kv5.at[rows_of(t)], buf.at[slot_no, rows_of(t)], hop_send.at[0, t], hop_recv.at[rk, t], partner).wait_recv()
                 return carry
-            lax.fori_loop(0, n, one, 0)
+            lax.fori_loop(start, stop, one, 0)
 
     gives = jnp.logical_or(me == 3, jnp.logical_or(me == 5, me == 1))
     spread = [(gives, send(last, last, last_send.at[0], last_recv, partner)), (me == 3, send(last, last, last_send.at[1], last_recv, xnb))]
@@ -410,6 +410,38 @@
                 on(c, cp, 'start')
 
     pass_last(jnp.logical_and(gives, me > 1))
+
+    pass_six = send(buf.at[5], buf.at[5], pass_send.at[5], wide_recv.at[5], partner)
+    pass_three = send(buf.at[3], buf.at[4], pass_send.at[3], wide_recv.at[4], partner)
+    gets_six = jnp.logical_and(helper, core == 0)
+
+    def attend_lent():
+        chunks_in(True, 5 + core, 3, 0, 1)
+        lend.wait_recv()
+        attend(buf[5 + core, 0:LENT, 0:HEAD], buf[5 + core, 0:LENT, HEAD:2 * HEAD], borrowed, LENT, True, True)
+
+        def block(k, carry):
+            s = jnp.where(k == 0, OWN, jnp.where(k <= 4, k - 1, jnp.where(k == 5, 5, 4)))
+            chunks_in(jnp.logical_and(k == 1, core == 0), 0, 0)
+            early = jnp.logical_and(k == 3, core == 0)
+            chunks_in(early, 5, 3, 1)
+            on(early, pass_six, 'start')
+            turn = k == 4
+            chunks_in(turn, 3, 2)
+            on(turn, pass_three, 'start')
+            on(jnp.logical_and(k == 5, core == 1), pass_six, 'wait_recv')
+            on(k == 6, pass_three, 'wait_recv')
+
+            @pl.when(jnp.logical_or(k != 5, core == 1))
+            def _():
+                attend(buf[s, :, 0:HEAD], buf[s, :, HEAD:2 * HEAD], borrowed, TOK, False, False)
+            return carry
+
+        lax.fori_loop(0, 7, block, 0)
+        for h in range(4):
+            total = jnp.sum(l[h, borrowed, :], axis=1, keepdims=True)
+            lent[h] = (acc[h, borrowed, :] / total).astype(BF16)
+        give_back.start()
 
     def step(s, carry):
         chunks_in(jnp.logical_and(s == 0, core == 1), 0, 0)
@@ -432,6 +464,10 @@
 
         for cond, cp in relay(s):
             on(cond, cp, 'start')
+
+        @pl.when(jnp.logical_and(helper, s == 2))
+        def _():
+            attend_lent()
 
         @pl.when(jnp.logical_or(s >= 1, core == 1))
         def _():
@@ -451,38 +487,6 @@
     lax.fori_loop(0, 2 * chip + 1, step, 0)
     pass_last(me == 1)
 
-    pass_six = send(buf.at[5], buf.at[5], pass_send.at[5], wide_recv.at[5], partner)
-    pass_three = send(buf.at[3], buf.at[4], pass_send.at[3], wide_recv.at[4], partner)
-    gets_six = jnp.logical_and(helper, core == 0)
-
-    @pl.when(helper)
-    def _():
-        chunks_in(core == 0, 5, 3)
-        chunks_in(core == 1, 6, 3, 1)
-        on(core == 0, pass_six, 'start')
-        chunks_in(core == 1, 3, 2)
-        on(core == 1, pass_three, 'start')
-        lend.wait_recv()
-        attend(buf[5 + core, 0:LENT, 0:HEAD], buf[5 + core, 0:LENT, HEAD:2 * HEAD], borrowed, LENT, True, True)
-
-        def block(k, carry):
-            s = jnp.where(k == 0, OWN, jnp.where(k <= 4, k - 1, jnp.where(k == 5, 5, 4)))
-            chunks_in(jnp.logical_and(k == 1, core == 0), 0, 0)
-            chunks_in(jnp.logical_and(k == 4, core == 0), 3, 2)
-            on(jnp.logical_and(k == 4, core == 0), pass_three, 'start')
-            on(jnp.logical_and(k == 5, core == 1), pass_six, 'wait_recv')
-            on(k == 6, pass_three, 'wait_recv')
-
-            @pl.when(jnp.logical_or(k != 5, core == 1))
-            def _():
-                attend(buf[s, :, 0:HEAD], buf[s, :, HEAD:2 * HEAD], borrowed, TOK, False, False)
-            return carry
-
-        lax.fori_loop(0, 7, block, 0)
-        for h in range(4):
-            total = jnp.sum(l[h, borrowed, :], axis=1, keepdims=True)
-            lent[h] = (acc[h, borrowed, :] / total).astype(BF16)
-        give_back.start()
 
     @pl.when(jnp.logical_and(jnp.logical_not(gives), jnp.logical_not(is_last)))
     def _():

time: 89.5 us -> 88.7 us (level)
  no operation moved by 1% of the time
where the time goes in v2:
time: 88.7 us; the launch traced here: 88.6 us
  Pallas kernels  84.3 us (95%)
  local copies, waits for them, and re-layouts  2.63 us (3%)
  between operations  1.44 us (2%)
    pallas_call x1, Pallas kernels, layers(): pl.pallas_call(functools.partial(layers_kernel, fast), in_specs=[anyw] *...  81.1 us
    pallas_call x1, Pallas kernels, emit(): pl.pallas_call(emit_kernel, in_specs=[anyw] * 5, out_specs=[anyw] * 5, ou...  3.15 us
    unnamed x9, local copies, waits for them, and re-layouts  2.63 us

profile of v2, /device:TPU:7, one launch (start us, length us, event | category | flops | bytes accessed | tf_op | source)
XLA Modules:
  0.0 88.6 jit_solution(2830759258647946301)
XLA Ops:
  0.6 0.0 copy-start
  0.6 0.0 copy-start.2
  0.7 0.0 copy-start.3
  0.7 0.0 copy-start.4
  0.7 2.2 %copy.21 = bf16[2,640,4,256]{3,1,2,0:T(8,128)(2,1)S(1)} copy(bf16[2,640,4,256]{3,2,1,0:T(4,128)(2,1)} %param.19) | data formatting | bytes 5242880 | tf_op args[3]
  2.9 0.2 copy-done
  3.2 0.1 copy-done.2
  3.3 0.0 copy-done.3
  3.3 0.0 copy-done.4
  3.3 81.1 %layers_fast.1 = (bf16[1024,640]{1,0:T(8,128)(2,1)}, bf16[1024,256]{1,0:T(8,128)(2,1)}, bf16[1024,256]{1,0:T(8,128)(2,1)}, bf16[1024,256]{1,0:T(8,128)(2,1)}, bf16[1024,256]{1,0:T(8,128)(2,1)}, /*index=5*/f32[1]{0:T(128)}) custom-call(f32[2,4,640]{2,1,0:T(4,128)S(1)} %copy-done.3, f32[2,2,256]{2,1,0:T(2,128)S(1)} %copy-done.4, ...), custom_call_target="tpu_custom_call" | custom-call | flops 60000002048 | bytes 31457280 | tf_op jit(solution)/shard_map/layers_fast/pallas_call | solution.py:565
  85.0 0.2 while.18
  85.2 3.1 %emit.1 = (bf16[1024,640]{1,0:T(8,128)(2,1)}, bf16[1024,256]{1,0:T(8,128)(2,1)}, bf16[1024,256]{1,0:T(8,128)(2,1)}, bf16[1024,256]{1,0:T(8,128)(2,1)}, bf16[1024,256]{1,0:T(8,128)(2,1)}) custom-call(bf16[1024,640]{1,0:T(8,128)(2,1)} %get-tuple-element.289, bf16[1024,256]{1,0:T(8,128)(2,1)} %get-tuple-element.290, bf16[1024,256]{1,0:T(8,128)(2,1)} %get-tuple-element.291, ...), custom_call_target="tpu_custom_call" | custom-call | tf_op jit(solution)/shard_map/emit/pallas_call | solution.py:601
Async XLA Ops:
  0.6 2.5 %copy-start = (bf16[2,4,256,640]{3,2,1,0:T(8,128)(2,1)S(1)}, bf16[2,4,256,640]{3,2,1,0:T(8,128)(2,1)}, u32[]{:S(2)}) copy-start(bf16[2,4,256,640]{3,2,1,0:T(8,128)(2,1)} %param.22) | copy-start | bytes 7864324
  0.6 2.7 %copy-start.2 = (bf16[2,640,1,256]{3,1,2,0:T(8,128)(2,1)S(1)}, bf16[2,640,1,256]{3,1,2,0:T(8,128)(2,1)}, u32[]{:S(2)}) copy-start(bf16[2,640,1,256]{3,1,2,0:T(8,128)(2,1)} %param.20) | copy-start | bytes 1966084
  0.7 2.6 %copy-start.3 = (f32[2,4,640]{2,1,0:T(4,128)S(1)}, f32[2,4,640]{2,1,0:T(4,128)}, u32[]{:S(2)}) copy-start(f32[2,4,640]{2,1,0:T(4,128)} %ng_hbm.1) | copy-start | bytes 61444
  0.7 2.6 %copy-start.4 = (f32[2,2,256]{2,1,0:T(2,128)S(1)}, f32[2,2,256]{2,1,0:T(2,128)}, u32[]{:S(2)}) copy-start(f32[2,2,256]{2,1,0:T(2,128)} %qg_hbm.1) | copy-start | bytes 12292

commit v3 on v2

--- a/solution.py
+++ b/solution.py
@@ -75,8 +75,8 @@
 OWN = 7
 LENT = 256
 N_TILE = TOK // TILE
-QROWS = 512
-FROWS = 512
+QROWS = 1024
+FROWS = 256
 PARTS = 2
 
 

time: 88.7 us -> 89 us (level)
  the two profiles are of different devices: /device:TPU:7 before, /device:TPU:3 now
where the time goes in v3:
time: 89 us; the launch traced here: 88.9 us
  Pallas kernels  84.8 us (95%)
  local copies, waits for them, and re-layouts  2.63 us (3%)
  between operations  1.44 us (2%)
    pallas_call x1, Pallas kernels, layers(): pl.pallas_call(functools.partial(layers_kernel, fast), in_specs=[anyw] *...  81.7 us
    pallas_call x1, Pallas kernels, emit(): pl.pallas_call(emit_kernel, in_specs=[anyw] * 5, out_specs=[anyw] * 5, ou...  3.15 us
    unnamed x9, local copies, waits for them, and re-layouts  2.63 us

profile of v3, /device:TPU:3, one launch (start us, length us, event | category | flops | bytes accessed | tf_op | source)
XLA Modules:
  0.0 88.9 jit_solution(8949150347239649407)
XLA Ops:
  0.6 0.0 copy-start
  0.6 0.0 copy-start.2
  0.7 0.0 copy-start.3
  0.7 0.0 copy-start.4
  0.7 2.2 %copy.21 = bf16[2,640,4,256]{3,1,2,0:T(8,128)(2,1)S(1)} copy(bf16[2,640,4,256]{3,2,1,0:T(4,128)(2,1)} %param.19) | data formatting | bytes 5242880 | tf_op args[3]
  2.9 0.2 copy-done
  3.2 0.1 copy-done.2
  3.3 0.0 copy-done.3
  3.3 0.0 copy-done.4
  3.3 81.7 %layers_fast.1 = (bf16[1024,640]{1,0:T(8,128)(2,1)}, bf16[1024,256]{1,0:T(8,128)(2,1)}, bf16[1024,256]{1,0:T(8,128)(2,1)}, bf16[1024,256]{1,0:T(8,128)(2,1)}, bf16[1024,256]{1,0:T(8,128)(2,1)}, /*index=5*/f32[1]{0:T(128)}) custom-call(f32[2,4,640]{2,1,0:T(4,128)S(1)} %copy-done.3, f32[2,2,256]{2,1,0:T(2,128)S(1)} %copy-done.4, ...), custom_call_target="tpu_custom_call" | custom-call | flops 60000002048 | bytes 31457280 | tf_op jit(solution)/shard_map/layers_fast/pallas_call | solution.py:565
  85.6 3.1 %emit.1 = (bf16[1024,640]{1,0:T(8,128)(2,1)}, bf16[1024,256]{1,0:T(8,128)(2,1)}, bf16[1024,256]{1,0:T(8,128)(2,1)}, bf16[1024,256]{1,0:T(8,128)(2,1)}, bf16[1024,256]{1,0:T(8,128)(2,1)}) custom-call(bf16[1024,640]{1,0:T(8,128)(2,1)} %get-tuple-element.289, bf16[1024,256]{1,0:T(8,128)(2,1)} %get-tuple-element.290, bf16[1024,256]{1,0:T(8,128)(2,1)} %get-tuple-element.291, ...), custom_call_target="tpu_custom_call" | custom-call | tf_op jit(solution)/shard_map/emit/pallas_call | solution.py:601
  (1 shorter events, 0.0 us)
Async XLA Ops:
  0.6 2.5 %copy-start = (bf16[2,4,256,640]{3,2,1,0:T(8,128)(2,1)S(1)}, bf16[2,4,256,640]{3,2,1,0:T(8,128)(2,1)}, u32[]{:S(2)}) copy-start(bf16[2,4,256,640]{3,2,1,0:T(8,128)(2,1)} %param.22) | copy-start | bytes 7864324
  0.6 2.7 %copy-start.2 = (bf16[2,640,1,256]{3,1,2,0:T(8,128)(2,1)S(1)}, bf16[2,640,1,256]{3,1,2,0:T(8,128)(2,1)}, u32[]{:S(2)}) copy-start(bf16[2,640,1,256]{3,1,2,0:T(8,128)(2,1)} %param.20) | copy-start | bytes 1966084
  0.7 2.6 %copy-start.3 = (f32[2,4,640]{2,1,0:T(4,128)S(1)}, f32[2,4,640]{2,1,0:T(4,128)}, u32[]{:S(2)}) copy-start(f32[2,4,640]{2,1,0:T(4,128)} %ng_hbm.1) | copy-start | bytes 61444
  0.7 2.6 %copy-start.4 = (f32[2,2,256]{2,1,0:T(2,128)S(1)}, f32[2,2,256]{2,1,0:T(2,128)}, u32[]{:S(2)}) copy-start(f32[2,2,256]{2,1,0:T(2,128)} %qg_hbm.1) | copy-start | bytes 12292
